TPU v7x, 32 devices: a whole 2x2x4 slice. The times are simulated.
32 devices in a mesh: wide: 8 (over y, x, core), narrow: 4 (over z).
Axes of the slice: x: 2, y: 2, z: 4, core: 2. Of those that a mesh axis runs over, the one named last changes fastest.
Arguments:
- schur_matrix: bfloat16 [8, 4, 3, 1024, 1024], P('wide', 'narrow')
- face_inverse: bfloat16 [8, 4, 3, 8, 128, 128], P('wide', 'narrow')
- deluxe: bfloat16 [8, 4, 3, 8, 128, 128], P('wide', 'narrow')
- primal_weight: float32 [8, 4, 3, 8, 128], P('wide', 'narrow'), may hold values from 0.05 to 0.3
- coarse_group: float32 [8, 96, 96], P('wide', 'narrow')
- coarse_map: float32 [8, 96, 8], P('wide', 'narrow'), may hold values from -0.625 to 0.625
- coarse_top: float32 [64, 64], P('wide')
- load_vector: bfloat16 [8, 4, 3, 8, 128, 128], P('wide', 'narrow'), may hold values from -6 to 6
- previous: bfloat16 [8, 4, 3, 8, 128, 128], P('wide', 'narrow'), may hold values from -3 to 3
- slot_count: int32 [8, 4], P('wide', 'narrow'), may hold values from 1 to 3, as said below
- partner: int32 [8, 4, 3, 8], P('wide', 'narrow'), may hold values from -1 to 2, as said below
- face_size: int32 [8, 4, 3, 8], P('wide', 'narrow'), may hold values from 0 to 128, as said below
Outputs:
- solution: float32 [8, 4, 3, 8, 128, 128], P('wide', 'narrow')
- residual: float32 [8, 4, 3, 8, 128, 128], P('wide', 'narrow')
Inputs may be any that keep to these rules, and one draw needn't show every extreme that they name: Slots of a device below its slot_count hold subdomains; the others are empty. `face_size`: both sides of a face with a partner have the same size; faces of empty slots have size 0, all other faces at least 32.
All inputs are finite; a program needn't handle non-finite values.
Results may differ from a plain program's by a relative error of at most 0.00355.
The roundings to bfloat16 on the way count: a program that leaves them out, or rounds other values in their place, can miss the bound.
Values may be sent and summed in bfloat16 or wider, within the bound.
No kernel may reach another device: no remote copies, remote signals or barrier semaphores. Data moves between devices by JAX's collectives and lax.ppermute only.
A program may use at most 128 MiB of HBM per device.

v0:
```python
import jax
import jax.numpy as jnp
from jax import lax
from jax.sharding import PartitionSpec as P

ITERS = 2
precise = lax.Precision.HIGHEST


def with_halo(block, sides, width, periodic):
    for axis, dim in sides:
        count = lax.axis_size(axis)
        forward = [(i, i + 1) for i in range(count - 1)]
        if periodic:
            forward.append((count - 1, 0))
        backward = [(target, source) for source, target in forward]
        low = lax.ppermute(
            lax.slice_in_dim(block, block.shape[dim] - width, None, axis=dim), axis, forward
        )
        high = lax.ppermute(lax.slice_in_dim(block, 0, width, axis=dim), axis, backward)
        block = jnp.concatenate([low, block, high], axis=dim)
    return block


def pick_partner(sources, partner):
    slot_total = sources.shape[1]
    chosen = partner[:, :, None] == jnp.arange(slot_total, dtype=jnp.int32)[None, None, :]
    spread = jnp.where(chosen[:, :, :, None, None], sources[None], jnp.zeros((), sources.dtype))
    return jnp.sum(spread, axis=2)


def face_sources(values, wide_got, narrow_got):
    return jnp.stack(
        [
            narrow_got[0],
            narrow_got[3],
            wide_got[0],
            wide_got[3],
            values[:, 5],
            values[:, 4],
            values[:, 7],
            values[:, 6],
        ],
        axis=0,
    )


def partner_full(values, partner):
    wide_got = with_halo(jnp.stack([values[:, 2], values[:, 3]], axis=0), (("wide", 0),), 1, True)
    narrow_got = with_halo(
        jnp.stack([values[:, 0], values[:, 1]], axis=0), (("narrow", 0),), 1, False
    )
    return pick_partner(face_sources(values, wide_got, narrow_got), partner)


def partner_half(values, partner):
    wide_got = with_halo(jnp.stack([values[:, 2], values[:, 3]], axis=0), (("wide", 0),), 1, True)
    narrow_got = with_halo(
        jnp.stack([values[:, 0], values[:, 1]], axis=0), (("narrow", 0),), 1, False
    )
    return pick_partner(face_sources(values, wide_got, narrow_got), partner)


def body(
    schur_matrix,
    face_inverse,
    deluxe,
    primal_weight,
    coarse_group,
    coarse_map,
    coarse_top,
    load_vector,
    previous,
    slot_count,
    partner,
    face_size,
):
    schur_matrix = schur_matrix[0, 0]
    face_inverse = face_inverse[0, 0]
    deluxe = deluxe[0, 0]
    primal_weight = primal_weight[0, 0]
    coarse_group = coarse_group[0]
    coarse_map = coarse_map[0]
    load_vector = load_vector[0, 0]
    previous = previous[0, 0]
    live_count = slot_count[0, 0]
    partner = partner[0, 0]
    face_size = face_size[0, 0]
    slot_total, face_total, face_width, columns = load_vector.shape
    block_order = schur_matrix.shape[1]
    slot_alive = jnp.arange(slot_total, dtype=jnp.int32)[:, None, None] < live_count
    inside = jnp.arange(face_width, dtype=jnp.int32)[None, None, :] < face_size[:, :, None]
    live_mask = jnp.where(jnp.logical_and(slot_alive, inside), 1.0, 0.0).astype(jnp.float32)[
        ..., None
    ]
    linked = (partner >= 0)[:, :, None, None]

    def global_inner(first_vec, second_vec, weights):
        return lax.psum(
            jnp.sum(weights * first_vec * second_vec, axis=(0, 1, 2)), ("wide", "narrow")
        )

    def operator(values):
        direction_half = values.astype(jnp.bfloat16)
        stacked = direction_half.reshape(slot_total, block_order, columns)
        result = jnp.einsum(
            "sij,sjr->sir", schur_matrix, stacked, preferred_element_type=jnp.float32
        )
        return live_mask * result.reshape(values.shape)

    def precondition(values):
        res_half = values.astype(jnp.bfloat16)
        scaled = live_mask * jnp.einsum(
            "sfkj,sfkr->sfjr", deluxe, res_half, preferred_element_type=jnp.float32
        )
        scaled_half = scaled.astype(jnp.bfloat16)
        local_part = jnp.einsum(
            "sfjk,sfkr->sfjr", face_inverse, scaled_half, preferred_element_type=jnp.float32
        )
        coarse_in = jnp.sum(primal_weight[..., None] * scaled, axis=2).reshape(
            slot_total * face_total, columns
        )
        group_vec = lax.all_gather(coarse_in, "narrow", axis=0, tiled=True)
        group_part = jnp.dot(coarse_group, group_vec, precision=precise)
        restricted = lax.psum(jnp.dot(coarse_map.T, coarse_in, precision=precise), "narrow")
        everyone = lax.all_gather(restricted, "wide", axis=0, tiled=True)
        top_part = jnp.dot(coarse_top, everyone, precision=precise)
        coarse_out = group_part + jnp.dot(coarse_map, top_part, precision=precise)
        correction = local_part + primal_weight[..., None] * coarse_out.reshape(
            slot_total, face_total, 1, columns
        )
        corr_half = (live_mask * correction).astype(jnp.bfloat16)
        weighted = live_mask * jnp.einsum(
            "sfjk,sfkr->sfjr", deluxe, corr_half, preferred_element_type=jnp.float32
        )
        assembled = weighted + partner_full(weighted, partner)
        return (assembled, weighted)

    def norm_of(values, weighted):
        return global_inner(values, weighted, 1.0)

    prev_full = previous.astype(jnp.float32)
    prev_partner = partner_half(previous, partner).astype(jnp.float32)
    averaged = live_mask * jnp.where(linked, 0.5 * (prev_full + prev_partner), prev_full)
    start_local = live_mask * load_vector.astype(jnp.float32) - operator(averaged)
    residual = start_local + partner_full(start_local, partner)
    solution = averaged
    precond, weighted = precondition(residual)
    precond_norm = norm_of(residual, weighted)
    direction = precond
    for iteration in range(ITERS):
        image_local = operator(direction)
        curvature = global_inner(direction, image_local, 1.0)
        image_full = image_local + partner_full(image_local, partner)
        step_size = precond_norm / curvature
        solution = solution + step_size * direction
        residual = residual - step_size * image_full
        if iteration + 1 < ITERS:
            precond, weighted = precondition(residual)
            next_norm = norm_of(residual, weighted)
            direction = precond + next_norm / precond_norm * direction
            precond_norm = next_norm
    return (solution[None, None], residual[None, None])


def solution(mesh):
    in_specs = (
        P("wide", "narrow", None, None, None),
        P("wide", "narrow", None, None, None, None),
        P("wide", "narrow", None, None, None, None),
        P("wide", "narrow", None, None, None),
        P("wide", "narrow", None),
        P("wide", "narrow", None),
        P("wide", None),
        P("wide", "narrow", None, None, None, None),
        P("wide", "narrow", None, None, None, None),
        P("wide", "narrow"),
        P("wide", "narrow", None, None),
        P("wide", "narrow", None, None),
    )
    out_specs = (
        P("wide", "narrow", None, None, None, None),
        P("wide", "narrow", None, None, None, None),
    )
    return jax.shard_map(body, mesh=mesh, in_specs=in_specs, out_specs=out_specs, check_vma=False)
```

profile of v0, /device:TPU:0, one launch (start us, length us, event | category | flops | bytes accessed | tf_op | source)
XLA Modules:
  0.0 334.1 jit_solution(3498991599465272584)
XLA Ops:
  1.8 3.4 %collective-permute-start.3 = (bf16[1,3,128,128]{3,2,1,0:T(8,128)(2,1)S(1)}, bf16[1,3,128,128]{3,2,1,0:T(8,128)(2,1)}, u32[]{:S(2)}, u32[]{:S(2)}) collective-permute-start(bf16[1,3,128,128]{3,2,1,0:T(8,128)(2,1)S(1)} %get-tuple-element.33), channel_id=1, source_target_pairs={{4,0},{8,4},{12,8},{16,12},{20,16},{24,20},{28,24},{0,28},{5,1},{9... | collective-permute-start | bytes 294920 | tf_op jit(solution)/shard_map/ppermute | solution.py:20
  6.5 5.2 %collective-permute-start = (bf16[1,3,128,128]{3,2,1,0:T(8,128)(2,1)S(1)}, bf16[1,3,128,128]{3,2,1,0:T(8,128)(2,1)}, u32[]{:S(2)}, u32[]{:S(2)}) collective-permute-start(bf16[1,3,128,128]{3,2,1,0:T(8,128)(2,1)S(1)} %get-tuple-element.36), channel_id=1, source_target_pairs={{0,1},{1,2},{2,3},{4,5},{5,6},{6,7},{8,9},{9,10},{10,11},{12,13},{... | collective-permute-start | bytes 294920 | tf_op jit(solution)/shard_map/ppermute | solution.py:17
  23.3 6.6 %fusion.23 = f32[3,1024,128]{1,2,0:T(8,128)} fusion(bf16[1,1,3,1024,1024]{4,3,2,1,0:T(8,128)(2,1)} %param.12, f32[3,1024,128]{1,2,0:T(8,128)S(1)} %copy.131, f32[3,1024,128]{1,2,0:T(8,128)} %copy.132, f32[3,1024]{1,0:T(4,128)S(1)} %copy-done.29, pred[3,1024]{1,0:T(4,128)(4,1)S(1)} %bitcast.426), kind=kOutput, calls=%fused_computation.50 | convolution fusion | flops 807272448 | bytes 11025408 | tf_op jit(solution)/shard_map/sij,sjr->sir/dot_general | solution.py:106
  39.5 4.6 %collective-permute-done.5 = f32[1,3,128,128]{3,2,1,0:T(8,128)S(1)} collective-permute-done((f32[1,3,128,128]{3,2,1,0:T(8,128)S(1)}, f32[1,3,128,128]{3,2,1,0:T(8,128)S(1)}, u32[]{:S(2)}, u32[]{:S(2)}) %collective-permute-start.5) | collective-permute-done | bytes 196640 | tf_op jit(solution)/shard_map/ppermute | solution.py:20
  49.2 12.1 %psum.42 = f32[8,128]{1,0:T(8,128)S(1)} all-reduce(f32[8,128]{1,0:T(8,128)S(1)} %convolution_bitcast_fusion.1), channel_id=1, replica_groups=mesh['wide'=8,'narrow'=4] {'narrow'}, use_global_device_ids=true, to_apply=%region_3.4 | all-reduce | flops 1024 | bytes 8192 | tf_op jit(solution)/shard_map/psum | solution.py:125
  61.3 8.1 %all_gather.13 = f32[64,128]{1,0:T(8,128)S(1)} all-gather(f32[8,128]{1,0:T(8,128)S(1)} %psum.42), channel_id=1, replica_groups=mesh['wide'=8,'narrow'=4] {'wide'}, dimensions={0}, use_global_device_ids=true | all-gather | bytes 36864 | tf_op jit(solution)/shard_map/all_gather | solution.py:126
  69.4 13.1 %all_gather.12 = f32[96,128]{1,0:T(8,128)S(1)} all-gather(f32[24,128]{1,0:T(8,128)S(1)} %bitcast.423), channel_id=1, replica_groups=mesh['wide'=8,'narrow'=4] {'narrow'}, dimensions={0}, use_global_device_ids=true | all-gather | bytes 61440 | tf_op jit(solution)/shard_map/all_gather | solution.py:123
  90.3 4.5 %collective-permute-done.9 = f32[1,3,128,128]{3,2,1,0:T(8,128)S(1)} collective-permute-done((f32[1,3,128,128]{3,2,1,0:T(8,128)S(1)}, f32[1,3,128,128]{3,2,1,0:T(8,128)S(1)}, u32[]{:S(2)}, u32[]{:S(2)}) %collective-permute-start.9) | collective-permute-done | bytes 196640 | tf_op jit(solution)/shard_map/ppermute | solution.py:20
  99.4 3.4 %fusion.26 = f32[3,1024,128]{1,2,0:T(8,128)} fusion(bf16[3,1024,128]{2,1,0:T(8,128)(2,1)S(1)} %bitcast.416, bf16[1,1,3,1024,1024]{4,3,2,1,0:T(8,128)(2,1)S(1)} %bitcast.400), kind=kOutput, calls=%fused_computation.51 | convolution fusion | flops 805306368 | bytes 8650752 | tf_op jit(solution)/shard_map/sij,sjr->sir/dot_general | solution.py:106
  102.8 3.0 copy.153
  109.8 5.4 %collective-permute-start.12 = (f32[1,3,128,128]{3,2,1,0:T(8,128)}, f32[1,3,128,128]{3,2,1,0:T(8,128)}, u32[]{:S(2)}, u32[]{:S(2)}) collective-permute-start(f32[1,3,128,128]{3,2,1,0:T(8,128)} %get-tuple-element.24), channel_id=1, source_target_pairs={{0,1},{1,2},{2,3},{4,5},{5,6},{6,7},{8,9},{9,10},{10,11},{12,13},{... | collective-permute-start | bytes 589832 | tf_op jit(solution)/shard_map/ppermute | solution.py:17
  117.0 40.9 %all-reduce = (f32[128]{0:T(128)S(1)}, f32[128]{0:T(128)S(1)}) all-reduce(f32[128]{0:T(128)S(1)} %get-tuple-element.20, f32[128]{0:T(128)S(1)} %get-tuple-element.8), channel_id=1, replica_groups=mesh['wide'=8,'narrow'=4] {'wide','narrow'}, use_global_device_ids=true, to_apply=%region_5.6 | all-reduce | flops 256 | bytes 2048 | tf_op jit(solution)/shard_map/psum | solution.py:99
  165.9 10.2 %psum.45 = f32[8,128]{1,0:T(8,128)S(1)} all-reduce(f32[8,128]{1,0:T(8,128)S(1)} %convolution_bitcast_fusion), channel_id=1, replica_groups=mesh['wide'=8,'narrow'=4] {'narrow'}, use_global_device_ids=true, to_apply=%region_11.12 | all-reduce | flops 1024 | bytes 8192 | tf_op jit(solution)/shard_map/psum | solution.py:125
  176.1 9.9 %all_gather.15 = f32[64,128]{1,0:T(8,128)S(1)} all-gather(f32[8,128]{1,0:T(8,128)S(1)} %psum.45), channel_id=1, replica_groups=mesh['wide'=8,'narrow'=4] {'wide'}, dimensions={0}, use_global_device_ids=true | all-gather | bytes 36864 | tf_op jit(solution)/shard_map/all_gather | solution.py:126
  186.1 13.1 %all_gather.14 = f32[96,128]{1,0:T(8,128)S(1)} all-gather(f32[24,128]{1,0:T(8,128)S(1)} %bitcast.422), channel_id=1, replica_groups=mesh['wide'=8,'narrow'=4] {'narrow'}, dimensions={0}, use_global_device_ids=true | all-gather | bytes 61440 | tf_op jit(solution)/shard_map/all_gather | solution.py:123
  199.6 4.4 %multiply_reduce_fusion.1 = (f32[128]{0:T(128)}, f32[3,8,128,128]{3,2,1,0:T(8,128)}) fusion(f32[3,8,128,128]{3,2,1,0:T(8,128)} %copy-done.20, bf16[1,1,3,8,128,128]{5,4,3,2,1,0:T(8,128)(2,1)S(1)} %copy-done.25, f32[3,8,128]{2,1,0:T(8,128)S(1)} %fusion.32, bf16[3,8,128,128]{2,3,1,0:T(8,128)(2,1)S(1)} %get-tuple-element.40, f32[3,8,128]{2,1,0:T(8,128)S(1)} %bitcast.421, ...), kind=kOutput, calls=%fused_computation.39 | convolution fusion | flops 204078976 | bytes 5542400 | tf_op jit(solution)/shard_map/sfjk,sfkr->sfjr/dot_general | solution.py:133
  209.4 40.3 %psum.46 = f32[128]{0:T(128)S(1)} all-reduce(f32[128]{0:T(128)S(1)} %copy-done.38), channel_id=1, replica_groups=mesh['wide'=8,'narrow'=4] {'wide','narrow'}, use_global_device_ids=true, to_apply=%region_13.14 | all-reduce | flops 128 | bytes 1024 | tf_op jit(solution)/shard_map/psum | solution.py:99
  252.6 5.5 %collective-permute-done.18 = f32[1,3,128,128]{3,2,1,0:T(8,128)S(1)} collective-permute-done((f32[1,3,128,128]{3,2,1,0:T(8,128)S(1)}, f32[1,3,128,128]{3,2,1,0:T(8,128)S(1)}, u32[]{:S(2)}, u32[]{:S(2)}) %collective-permute-start.18) | collective-permute-done | bytes 196640 | tf_op jit(solution)/shard_map/ppermute | solution.py:17
  263.1 3.4 %fusion.29 = f32[3,1024,128]{1,2,0:T(8,128)} fusion(bf16[3,1024,128]{2,1,0:T(8,128)(2,1)S(1)} %bitcast.417, bf16[1,1,3,1024,1024]{4,3,2,1,0:T(8,128)(2,1)S(1)} %bitcast.402), kind=kOutput, calls=%fused_computation.52 | convolution fusion | flops 805306368 | bytes 8650752 | tf_op jit(solution)/shard_map/sij,sjr->sir/dot_general | solution.py:106
  269.5 3.2 multiply_reduce_fusion
  272.7 38.1 %psum.47 = f32[128]{0:T(128)S(1)} all-reduce(f32[128]{0:T(128)S(1)} %get-tuple-element.4), channel_id=1, replica_groups=mesh['wide'=8,'narrow'=4] {'wide','narrow'}, use_global_device_ids=true, to_apply=%region_16.17 | all-reduce | flops 128 | bytes 1024 | tf_op jit(solution)/shard_map/psum | solution.py:99
  313.4 4.6 %collective-permute-start.20 = (f32[1,3,128,128]{3,2,1,0:T(8,128)S(1)}, f32[1,3,128,128]{3,2,1,0:T(8,128)S(1)}, u32[]{:S(2)}, u32[]{:S(2)}) collective-permute-start(f32[1,3,128,128]{3,2,1,0:T(8,128)S(1)} %get-tuple-element.15), channel_id=1, source_target_pairs={{0,1},{1,2},{2,3},{4,5},{5,6},{6,7},{8,9},{9,10},{10,11},{12,13},{... | collective-permute-start | bytes 589832 | tf_op jit(solution)/shard_map/ppermute | solution.py:17
  318.1 3.1 fusion.10
  321.8 7.8 %collective-permute-done.22 = f32[1,3,128,128]{3,2,1,0:T(8,128)S(1)} collective-permute-done((f32[1,3,128,128]{3,2,1,0:T(8,128)S(1)}, f32[1,3,128,128]{3,2,1,0:T(8,128)S(1)}, u32[]{:S(2)}, u32[]{:S(2)}) %collective-permute-start.22) | collective-permute-done | bytes 196640 | tf_op jit(solution)/shard_map/ppermute | solution.py:17
  (232 shorter events, 77.9 us)
Async XLA Ops:
  1.8 18.4 %collective-permute-start.3 = (bf16[1,3,128,128]{3,2,1,0:T(8,128)(2,1)S(1)}, bf16[1,3,128,128]{3,2,1,0:T(8,128)(2,1)}, u32[]{:S(2)}, u32[]{:S(2)}) collective-permute-start(bf16[1,3,128,128]{3,2,1,0:T(8,128)(2,1)S(1)} %get-tuple-element.33), channel_id=1, source_target_pairs={{4,0},{8,4},{12,8},{16,12},{20,16},{24,20},{28,24},{0,28},{5,1},{9... | collective-permute-start | bytes 294920 | tf_op jit(solution)/shard_map/ppermute | solution.py:20
  5.2 14.1 %collective-permute-start.2 = (bf16[1,3,128,128]{3,2,1,0:T(8,128)(2,1)S(1)}, bf16[1,3,128,128]{3,2,1,0:T(8,128)(2,1)}, u32[]{:S(2)}, u32[]{:S(2)}) collective-permute-start(bf16[1,3,128,128]{3,2,1,0:T(8,128)(2,1)S(1)} %get-tuple-element.34), channel_id=1, source_target_pairs={{0,4},{4,8},{8,12},{12,16},{16,20},{20,24},{24,28},{28,0},{1,5},{5... | collective-permute-start | bytes 294920 | tf_op jit(solution)/shard_map/ppermute | solution.py:17
  5.2 13.2 %collective-permute-start.1 = (bf16[1,3,128,128]{3,2,1,0:T(8,128)(2,1)S(1)}, bf16[1,3,128,128]{3,2,1,0:T(8,128)(2,1)}, u32[]{:S(2)}, u32[]{:S(2)}) collective-permute-start(bf16[1,3,128,128]{3,2,1,0:T(8,128)(2,1)S(1)} %get-tuple-element.35), channel_id=1, source_target_pairs={{1,0},{2,1},{3,2},{5,4},{6,5},{7,6},{9,8},{10,9},{11,10},{13,12},{... | collective-permute-start | bytes 294920 | tf_op jit(solution)/shard_map/ppermute | solution.py:20
  6.5 11.0 %collective-permute-start = (bf16[1,3,128,128]{3,2,1,0:T(8,128)(2,1)S(1)}, bf16[1,3,128,128]{3,2,1,0:T(8,128)(2,1)}, u32[]{:S(2)}, u32[]{:S(2)}) collective-permute-start(bf16[1,3,128,128]{3,2,1,0:T(8,128)(2,1)S(1)} %get-tuple-element.36), channel_id=1, source_target_pairs={{0,1},{1,2},{2,3},{4,5},{5,6},{6,7},{8,9},{9,10},{10,11},{12,13},{... | collective-permute-start | bytes 294920 | tf_op jit(solution)/shard_map/ppermute | solution.py:17
  33.1 6.4 %collective-permute-start.4 = (f32[1,3,128,128]{3,2,1,0:T(8,128)S(1)}, f32[1,3,128,128]{3,2,1,0:T(8,128)S(1)}, u32[]{:S(2)}, u32[]{:S(2)}) collective-permute-start(f32[1,3,128,128]{3,2,1,0:T(8,128)S(1)} %get-tuple-element.32), channel_id=1, source_target_pairs={{0,1},{1,2},{2,3},{4,5},{5,6},{6,7},{8,9},{9,10},{10,11},{12,13},{... | collective-permute-start | bytes 589832 | tf_op jit(solution)/shard_map/ppermute | solution.py:17
  35.9 8.1 %collective-permute-start.5 = (f32[1,3,128,128]{3,2,1,0:T(8,128)S(1)}, f32[1,3,128,128]{3,2,1,0:T(8,128)S(1)}, u32[]{:S(2)}, u32[]{:S(2)}) collective-permute-start(f32[1,3,128,128]{3,2,1,0:T(8,128)S(1)} %get-tuple-element.31), channel_id=1, source_target_pairs={{1,0},{2,1},{3,2},{5,4},{6,5},{7,6},{9,8},{10,9},{11,10},{13,12},{... | collective-permute-start | bytes 589832 | tf_op jit(solution)/shard_map/ppermute | solution.py:20
  37.2 7.9 %collective-permute-start.7 = (f32[1,3,128,128]{3,2,1,0:T(8,128)S(1)}, f32[1,3,128,128]{3,2,1,0:T(8,128)S(1)}, u32[]{:S(2)}, u32[]{:S(2)}) collective-permute-start(f32[1,3,128,128]{3,2,1,0:T(8,128)S(1)} %get-tuple-element.29), channel_id=1, source_target_pairs={{4,0},{8,4},{12,8},{16,12},{20,16},{24,20},{28,24},{0,28},{5,1},{9... | collective-permute-start | bytes 589832 | tf_op jit(solution)/shard_map/ppermute | solution.py:20
  39.1 6.0 %collective-permute-start.6 = (f32[1,3,128,128]{3,2,1,0:T(8,128)S(1)}, f32[1,3,128,128]{3,2,1,0:T(8,128)S(1)}, u32[]{:S(2)}, u32[]{:S(2)}) collective-permute-start(f32[1,3,128,128]{3,2,1,0:T(8,128)S(1)} %get-tuple-element.30), channel_id=1, source_target_pairs={{0,4},{4,8},{8,12},{12,16},{16,20},{20,24},{24,28},{28,0},{1,5},{5... | collective-permute-start | bytes 589832 | tf_op jit(solution)/shard_map/ppermute | solution.py:17
  85.5 4.7 %collective-permute-start.8 = (f32[1,3,128,128]{3,2,1,0:T(8,128)S(1)}, f32[1,3,128,128]{3,2,1,0:T(8,128)S(1)}, u32[]{:S(2)}, u32[]{:S(2)}) collective-permute-start(f32[1,3,128,128]{3,2,1,0:T(8,128)S(1)} %get-tuple-element.28), channel_id=1, source_target_pairs={{0,1},{1,2},{2,3},{4,5},{5,6},{6,7},{8,9},{9,10},{10,11},{12,13},{... | collective-permute-start | bytes 589832 | tf_op jit(solution)/shard_map/ppermute | solution.py:17
  87.1 7.7 %collective-permute-start.9 = (f32[1,3,128,128]{3,2,1,0:T(8,128)S(1)}, f32[1,3,128,128]{3,2,1,0:T(8,128)S(1)}, u32[]{:S(2)}, u32[]{:S(2)}) collective-permute-start(f32[1,3,128,128]{3,2,1,0:T(8,128)S(1)} %get-tuple-element.27), channel_id=1, source_target_pairs={{1,0},{2,1},{3,2},{5,4},{6,5},{7,6},{9,8},{10,9},{11,10},{13,12},{... | collective-permute-start | bytes 589832 | tf_op jit(solution)/shard_map/ppermute | solution.py:20
  88.5 7.3 %collective-permute-start.11 = (f32[1,3,128,128]{3,2,1,0:T(8,128)S(1)}, f32[1,3,128,128]{3,2,1,0:T(8,128)S(1)}, u32[]{:S(2)}, u32[]{:S(2)}) collective-permute-start(f32[1,3,128,128]{3,2,1,0:T(8,128)S(1)} %get-tuple-element.25), channel_id=1, source_target_pairs={{4,0},{8,4},{12,8},{16,12},{20,16},{24,20},{28,24},{0,28},{5,1},{9... | collective-permute-start | bytes 589832 | tf_op jit(solution)/shard_map/ppermute | solution.py:20
  88.6 7.2 %collective-permute-start.10 = (f32[1,3,128,128]{3,2,1,0:T(8,128)S(1)}, f32[1,3,128,128]{3,2,1,0:T(8,128)S(1)}, u32[]{:S(2)}, u32[]{:S(2)}) collective-permute-start(f32[1,3,128,128]{3,2,1,0:T(8,128)S(1)} %get-tuple-element.26), channel_id=1, source_target_pairs={{0,4},{4,8},{8,12},{12,16},{16,20},{20,24},{24,28},{28,0},{1,5},{5... | collective-permute-start | bytes 589832 | tf_op jit(solution)/shard_map/ppermute | solution.py:17
  109.8 48.2 %collective-permute-start.12 = (f32[1,3,128,128]{3,2,1,0:T(8,128)}, f32[1,3,128,128]{3,2,1,0:T(8,128)}, u32[]{:S(2)}, u32[]{:S(2)}) collective-permute-start(f32[1,3,128,128]{3,2,1,0:T(8,128)} %get-tuple-element.24), channel_id=1, source_target_pairs={{0,1},{1,2},{2,3},{4,5},{5,6},{6,7},{8,9},{9,10},{10,11},{12,13},{... | collective-permute-start | bytes 589832 | tf_op jit(solution)/shard_map/ppermute | solution.py:17
  115.2 43.8 %collective-permute-start.13 = (f32[1,3,128,128]{3,2,1,0:T(8,128)}, f32[1,3,128,128]{3,2,1,0:T(8,128)}, u32[]{:S(2)}, u32[]{:S(2)}) collective-permute-start(f32[1,3,128,128]{3,2,1,0:T(8,128)} %get-tuple-element.23), channel_id=1, source_target_pairs={{1,0},{2,1},{3,2},{5,4},{6,5},{7,6},{9,8},{10,9},{11,10},{13,12},{... | collective-permute-start | bytes 589832 | tf_op jit(solution)/shard_map/ppermute | solution.py:20
  116.4 44.4 %collective-permute-start.15 = (f32[1,3,128,128]{3,2,1,0:T(8,128)S(1)}, f32[1,3,128,128]{3,2,1,0:T(8,128)}, u32[]{:S(2)}, u32[]{:S(2)}) collective-permute-start(f32[1,3,128,128]{3,2,1,0:T(8,128)S(1)} %get-tuple-element.21), channel_id=1, source_target_pairs={{4,0},{8,4},{12,8},{16,12},{20,16},{24,20},{28,24},{0,28},{5,1},{9... | collective-permute-start | bytes 589832 | tf_op jit(solution)/shard_map/ppermute | solution.py:20
  116.5 43.4 %collective-permute-start.14 = (f32[1,3,128,128]{3,2,1,0:T(8,128)}, f32[1,3,128,128]{3,2,1,0:T(8,128)}, u32[]{:S(2)}, u32[]{:S(2)}) collective-permute-start(f32[1,3,128,128]{3,2,1,0:T(8,128)} %get-tuple-element.22), channel_id=1, source_target_pairs={{0,4},{4,8},{8,12},{12,16},{16,20},{20,24},{24,28},{28,0},{1,5},{5... | collective-permute-start | bytes 589832 | tf_op jit(solution)/shard_map/ppermute | solution.py:17
  206.1 44.6 %collective-permute-start.16 = (f32[1,3,128,128]{3,2,1,0:T(8,128)}, f32[1,3,128,128]{3,2,1,0:T(8,128)}, u32[]{:S(2)}, u32[]{:S(2)}) collective-permute-start(f32[1,3,128,128]{3,2,1,0:T(8,128)} %get-tuple-element.19), channel_id=1, source_target_pairs={{0,1},{1,2},{2,3},{4,5},{5,6},{6,7},{8,9},{9,10},{10,11},{12,13},{... | collective-permute-start | bytes 589832 | tf_op jit(solution)/shard_map/ppermute | solution.py:17
  208.1 43.6 %collective-permute-start.17 = (f32[1,3,128,128]{3,2,1,0:T(8,128)S(1)}, f32[1,3,128,128]{3,2,1,0:T(8,128)}, u32[]{:S(2)}, u32[]{:S(2)}) collective-permute-start(f32[1,3,128,128]{3,2,1,0:T(8,128)S(1)} %get-tuple-element.18), channel_id=1, source_target_pairs={{1,0},{2,1},{3,2},{5,4},{6,5},{7,6},{9,8},{10,9},{11,10},{13,12},{... | collective-permute-start | bytes 589832 | tf_op jit(solution)/shard_map/ppermute | solution.py:20
  249.8 8.4 %collective-permute-start.19 = (f32[1,3,128,128]{3,2,1,0:T(8,128)S(1)}, f32[1,3,128,128]{3,2,1,0:T(8,128)S(1)}, u32[]{:S(2)}, u32[]{:S(2)}) collective-permute-start(f32[1,3,128,128]{3,2,1,0:T(8,128)S(1)} %get-tuple-element.16), channel_id=1, source_target_pairs={{4,0},{8,4},{12,8},{16,12},{20,16},{24,20},{28,24},{0,28},{5,1},{9... | collective-permute-start | bytes 589832 | tf_op jit(solution)/shard_map/ppermute | solution.py:20
  250.7 7.4 %collective-permute-start.18 = (f32[1,3,128,128]{3,2,1,0:T(8,128)S(1)}, f32[1,3,128,128]{3,2,1,0:T(8,128)S(1)}, u32[]{:S(2)}, u32[]{:S(2)}) collective-permute-start(f32[1,3,128,128]{3,2,1,0:T(8,128)S(1)} %get-tuple-element.17), channel_id=1, source_target_pairs={{0,4},{4,8},{8,12},{12,16},{16,20},{20,24},{24,28},{28,0},{1,5},{5... | collective-permute-start | bytes 589832 | tf_op jit(solution)/shard_map/ppermute | solution.py:17
  312.1 9.6 %collective-permute-start.21 = (f32[1,3,128,128]{3,2,1,0:T(8,128)S(1)}, f32[1,3,128,128]{3,2,1,0:T(8,128)S(1)}, u32[]{:S(2)}, u32[]{:S(2)}) collective-permute-start(f32[1,3,128,128]{3,2,1,0:T(8,128)S(1)} %get-tuple-element.14), channel_id=1, source_target_pairs={{1,0},{2,1},{3,2},{5,4},{6,5},{7,6},{9,8},{10,9},{11,10},{13,12},{... | collective-permute-start | bytes 589832 | tf_op jit(solution)/shard_map/ppermute | solution.py:20
  313.4 8.3 %collective-permute-start.20 = (f32[1,3,128,128]{3,2,1,0:T(8,128)S(1)}, f32[1,3,128,128]{3,2,1,0:T(8,128)S(1)}, u32[]{:S(2)}, u32[]{:S(2)}) collective-permute-start(f32[1,3,128,128]{3,2,1,0:T(8,128)S(1)} %get-tuple-element.15), channel_id=1, source_target_pairs={{0,1},{1,2},{2,3},{4,5},{5,6},{6,7},{8,9},{9,10},{10,11},{12,13},{... | collective-permute-start | bytes 589832 | tf_op jit(solution)/shard_map/ppermute | solution.py:17
  321.2 8.3 %collective-permute-start.23 = (f32[1,3,128,128]{3,2,1,0:T(8,128)S(1)}, f32[1,3,128,128]{3,2,1,0:T(8,128)S(1)}, u32[]{:S(2)}, u32[]{:S(2)}) collective-permute-start(f32[1,3,128,128]{3,2,1,0:T(8,128)S(1)} %get-tuple-element.12), channel_id=1, source_target_pairs={{4,0},{8,4},{12,8},{16,12},{20,16},{24,20},{28,24},{0,28},{5,1},{9... | collective-permute-start | bytes 589832 | tf_op jit(solution)/shard_map/ppermute | solution.py:20
  321.5 8.0 %collective-permute-start.22 = (f32[1,3,128,128]{3,2,1,0:T(8,128)S(1)}, f32[1,3,128,128]{3,2,1,0:T(8,128)S(1)}, u32[]{:S(2)}, u32[]{:S(2)}) collective-permute-start(f32[1,3,128,128]{3,2,1,0:T(8,128)S(1)} %get-tuple-element.13), channel_id=1, source_target_pairs={{0,4},{4,8},{8,12},{12,16},{16,20},{20,24},{24,28},{28,0},{1,5},{5... | collective-permute-start | bytes 589832 | tf_op jit(solution)/shard_map/ppermute | solution.py:17
  (47 other events, 689.4 us)
where the time goes:
time: 336 us; the launch traced here: 334 us
  blocking collectives  186 us (55%)
  local copies, waits for them, and re-layouts  38.2 us (11%)
  starting transfers between devices  37.2 us (11%)
  waiting for transfers between devices  25.9 us (8%)
  matrix products  24.9 us (7%)
  other arithmetic  19.7 us (6%)
    psum x3, blocking collectives, global_inner(): lax.psum(jnp.sum(weights * first_vec * second_vec, axis=(0, 1, 2)), ('wid...  119 us
    all_gather x2, blocking collectives, precondition(): group_vec = lax.all_gather(coarse_in, 'narrow', axis=0, tiled=True)  26.2 us
    unnamed x141, local copies, waits for them, and re-layouts  23 us
    ppermute x12, starting transfers between devices, with_halo(): lax.ppermute(lax.slice_in_dim(block, block.shape[dim] - width, None, axis...  22.7 us
    psum x2, blocking collectives, precondition(): lax.psum(jnp.dot(coarse_map.T, coarse_in, precision=precise), 'narrow')  22.3 us
    all_gather x2, blocking collectives, precondition(): everyone = lax.all_gather(restricted, 'wide', axis=0, tiled=True)  18 us
    ppermute x12, waiting for transfers between devices, with_halo(): lax.ppermute(lax.slice_in_dim(block, block.shape[dim] - width, None, axis...  16.8 us
    ppermute x12, starting transfers between devices, with_halo(): lax.ppermute(lax.slice_in_dim(block, 0, width, axis=dim), axis, backward)  14.5 us
  transfers between devices with their start and end apart: 24, of which 8 were waited for; matrix products, arithmetic and copies ran while one was open for 5% of the time, Pallas kernels for 0%

commit v1 on v0

--- a/solution.py
+++ b/solution.py
@@ -122,7 +122,9 @@
         )
         group_vec = lax.all_gather(coarse_in, "narrow", axis=0, tiled=True)
         group_part = jnp.dot(coarse_group, group_vec, precision=precise)
-        restricted = lax.psum(jnp.dot(coarse_map.T, coarse_in, precision=precise), "narrow")
+        own = jnp.dot(coarse_map.T, coarse_in, precision=precise)
+        blocks = lax.all_gather(own, "narrow", axis=0, tiled=False)
+        restricted = blocks.sum(axis=0)
         everyone = lax.all_gather(restricted, "wide", axis=0, tiled=True)
         top_part = jnp.dot(coarse_top, everyone, precision=precise)
         coarse_out = group_part + jnp.dot(coarse_map, top_part, precision=precise)

time: 336 us -> 344 us (1.024)
  blocking collectives: 186 us -> 193 us
    all_gather x0 -> x2, blocking collectives: none -> 28.1 us  [precondition(): blocks = lax.all_gather(own, 'narrow', axis=0, tiled=False)]
    psum x2 -> x0, blocking collectives: 22.3 us -> none  [precondition(): lax.psum(jnp.dot(coarse_map.T, coarse_in, precision=precise), 'narrow')]
where the time goes in v1:
time: 344 us; the launch traced here: 343 us
  blocking collectives  193 us (56%)
  starting transfers between devices  38.4 us (11%)
  local copies, waits for them, and re-layouts  38.2 us (11%)
  waiting for transfers between devices  26.3 us (8%)
  matrix products  25.3 us (7%)
  other arithmetic  19.7 us (6%)
    psum x3, blocking collectives, global_inner(): lax.psum(jnp.sum(weights * first_vec * second_vec, axis=(0, 1, 2)), ('wid...  121 us
    all_gather x2, blocking collectives, precondition(): blocks = lax.all_gather(own, 'narrow', axis=0, tiled=False)  28.1 us
    all_gather x2, blocking collectives, precondition(): group_vec = lax.all_gather(coarse_in, 'narrow', axis=0, tiled=True)  26.1 us
    ppermute x12, starting transfers between devices, with_halo(): lax.ppermute(lax.slice_in_dim(block, block.shape[dim] - width, None, axis...  24 us
    unnamed x141, local copies, waits for them, and re-layouts  22.9 us
    all_gather x2, blocking collectives, precondition(): everyone = lax.all_gather(restricted, 'wide', axis=0, tiled=True)  17.9 us
    ppermute x12, waiting for transfers between devices, with_halo(): lax.ppermute(lax.slice_in_dim(block, block.shape[dim] - width, None, axis...  17.3 us
    ppermute x12, starting transfers between devices, with_halo(): lax.ppermute(lax.slice_in_dim(block, 0, width, axis=dim), axis, backward)  14.4 us
  transfers between devices with their start and end apart: 24, of which 8 were waited for; matrix products, arithmetic and copies ran while one was open for 5% of the time, Pallas kernels for 0%

profile of v1, /device:TPU:0, one launch (start us, length us, event | category | flops | bytes accessed | tf_op | source)
XLA Modules:
  0.0 343.1 jit_solution(13955799774175822417)
XLA Ops:
  1.8 3.4 collective-permute-start.3
  6.5 5.2 %collective-permute-start = (bf16[1,3,128,128]{3,2,1,0:T(8,128)(2,1)S(1)}, bf16[1,3,128,128]{3,2,1,0:T(8,128)(2,1)}, u32[]{:S(2)}, u32[]{:S(2)}) collective-permute-start(bf16[1,3,128,128]{3,2,1,0:T(8,128)(2,1)S(1)} %get-tuple-element.36), channel_id=1, source_target_pairs={{0,1},{1,2},{2,3},{4,5},{5,6},{6,7},{8,9},{9,10},{10,11},{12,13},{... | collective-permute-start | bytes 294920 | tf_op jit(solution)/shard_map/ppermute | solution.py:17
  23.3 6.6 %fusion.23 = f32[3,1024,128]{1,2,0:T(8,128)} fusion(bf16[1,1,3,1024,1024]{4,3,2,1,0:T(8,128)(2,1)} %param.12, f32[3,1024,128]{1,2,0:T(8,128)S(1)} %copy.76, f32[3,1024,128]{1,2,0:T(8,128)} %copy.77, f32[3,1024]{1,0:T(4,128)S(1)} %copy-done.29, pred[3,1024]{1,0:T(4,128)(4,1)S(1)} %bitcast.430), kind=kOutput, calls=%fused_computation.50 | convolution fusion | flops 807272448 | bytes 11025408 | tf_op jit(solution)/shard_map/sij,sjr->sir/dot_general | solution.py:106
  39.5 4.6 %collective-permute-done.5 = f32[1,3,128,128]{3,2,1,0:T(8,128)S(1)} collective-permute-done((f32[1,3,128,128]{3,2,1,0:T(8,128)S(1)}, f32[1,3,128,128]{3,2,1,0:T(8,128)S(1)}, u32[]{:S(2)}, u32[]{:S(2)}) %collective-permute-start.5) | collective-permute-done | bytes 196640 | tf_op jit(solution)/shard_map/ppermute | solution.py:20
  49.2 14.8 %all-gather = f32[32,128]{1,0:T(8,128)S(1)} all-gather(f32[8,128]{1,0:T(8,128)S(1)} %convolution_bitcast_fusion.1), channel_id=2, replica_groups=mesh['wide'=8,'narrow'=4] {'narrow'}, dimensions={0}, use_global_device_ids=true | all-gather | bytes 20480 | tf_op jit(solution)/shard_map/all_gather | solution.py:126
  64.0 8.1 %all_gather.27 = f32[64,128]{1,0:T(8,128)S(1)} all-gather(f32[8,128]{1,0:T(8,128)S(1)} %bitcast_reduce_fusion.1), channel_id=1, replica_groups=mesh['wide'=8,'narrow'=4] {'wide'}, dimensions={0}, use_global_device_ids=true | all-gather | bytes 36864 | tf_op jit(solution)/shard_map/all_gather | solution.py:128
  72.1 13.1 %all_gather.24 = f32[96,128]{1,0:T(8,128)S(1)} all-gather(f32[24,128]{1,0:T(8,128)S(1)} %bitcast.427), channel_id=1, replica_groups=mesh['wide'=8,'narrow'=4] {'narrow'}, dimensions={0}, use_global_device_ids=true | all-gather | bytes 61440 | tf_op jit(solution)/shard_map/all_gather | solution.py:123
  94.2 4.4 %collective-permute-done.9 = f32[1,3,128,128]{3,2,1,0:T(8,128)S(1)} collective-permute-done((f32[1,3,128,128]{3,2,1,0:T(8,128)S(1)}, f32[1,3,128,128]{3,2,1,0:T(8,128)S(1)}, u32[]{:S(2)}, u32[]{:S(2)}) %collective-permute-start.9) | collective-permute-done | bytes 196640 | tf_op jit(solution)/shard_map/ppermute | solution.py:20
  103.1 3.4 %fusion.26 = f32[3,1024,128]{1,2,0:T(8,128)} fusion(bf16[3,1024,128]{2,1,0:T(8,128)(2,1)S(1)} %bitcast.420, bf16[1,1,3,1024,1024]{4,3,2,1,0:T(8,128)(2,1)S(1)} %bitcast.404), kind=kOutput, calls=%fused_computation.51 | convolution fusion | flops 805306368 | bytes 8650752 | tf_op jit(solution)/shard_map/sij,sjr->sir/dot_general | solution.py:106
  106.6 3.0 copy.96
  113.6 5.4 %collective-permute-start.12 = (f32[1,3,128,128]{3,2,1,0:T(8,128)}, f32[1,3,128,128]{3,2,1,0:T(8,128)}, u32[]{:S(2)}, u32[]{:S(2)}) collective-permute-start(f32[1,3,128,128]{3,2,1,0:T(8,128)} %get-tuple-element.24), channel_id=1, source_target_pairs={{0,1},{1,2},{2,3},{4,5},{5,6},{6,7},{8,9},{9,10},{10,11},{12,13},{... | collective-permute-start | bytes 589832 | tf_op jit(solution)/shard_map/ppermute | solution.py:17
  120.8 41.0 %all-reduce = (f32[128]{0:T(128)S(1)}, f32[128]{0:T(128)S(1)}) all-reduce(f32[128]{0:T(128)S(1)} %get-tuple-element.20, f32[128]{0:T(128)S(1)} %get-tuple-element.8), channel_id=1, replica_groups=mesh['wide'=8,'narrow'=4] {'wide','narrow'}, use_global_device_ids=true, to_apply=%region_5.6 | all-reduce | flops 256 | bytes 2048 | tf_op jit(solution)/shard_map/psum | solution.py:99
  169.8 13.2 %all-gather.1 = f32[32,128]{1,0:T(8,128)S(1)} all-gather(f32[8,128]{1,0:T(8,128)S(1)} %convolution_bitcast_fusion), channel_id=3, replica_groups=mesh['wide'=8,'narrow'=4] {'narrow'}, dimensions={0}, use_global_device_ids=true | all-gather | bytes 20480 | tf_op jit(solution)/shard_map/all_gather | solution.py:126
  183.0 9.9 %all_gather.31 = f32[64,128]{1,0:T(8,128)S(1)} all-gather(f32[8,128]{1,0:T(8,128)S(1)} %bitcast_reduce_fusion), channel_id=1, replica_groups=mesh['wide'=8,'narrow'=4] {'wide'}, dimensions={0}, use_global_device_ids=true | all-gather | bytes 36864 | tf_op jit(solution)/shard_map/all_gather | solution.py:128
  193.2 13.1 %all_gather.28 = f32[96,128]{1,0:T(8,128)S(1)} all-gather(f32[24,128]{1,0:T(8,128)S(1)} %bitcast.426), channel_id=1, replica_groups=mesh['wide'=8,'narrow'=4] {'narrow'}, dimensions={0}, use_global_device_ids=true | all-gather | bytes 61440 | tf_op jit(solution)/shard_map/all_gather | solution.py:123
  206.7 4.4 %multiply_reduce_fusion.1 = (f32[128]{0:T(128)}, f32[3,8,128,128]{3,2,1,0:T(8,128)}) fusion(f32[3,8,128,128]{3,2,1,0:T(8,128)} %copy-done.20, bf16[1,1,3,8,128,128]{5,4,3,2,1,0:T(8,128)(2,1)S(1)} %copy-done.25, f32[3,8,128]{2,1,0:T(8,128)S(1)} %fusion.32, bf16[3,8,128,128]{2,3,1,0:T(8,128)(2,1)S(1)} %get-tuple-element.40, f32[3,8,128]{2,1,0:T(8,128)S(1)} %bitcast.425, ...), kind=kOutput, calls=%fused_computation.39 | convolution fusion | flops 204078976 | bytes 5542400 | tf_op jit(solution)/shard_map/sfjk,sfkr->sfjr/dot_general | solution.py:135
  216.8 40.3 %psum.30 = f32[128]{0:T(128)S(1)} all-reduce(f32[128]{0:T(128)S(1)} %copy-done.38), channel_id=1, replica_groups=mesh['wide'=8,'narrow'=4] {'wide','narrow'}, use_global_device_ids=true, to_apply=%region_13.14 | all-reduce | flops 128 | bytes 1024 | tf_op jit(solution)/shard_map/psum | solution.py:99
  260.1 6.1 %collective-permute-done.18 = f32[1,3,128,128]{3,2,1,0:T(8,128)S(1)} collective-permute-done((f32[1,3,128,128]{3,2,1,0:T(8,128)S(1)}, f32[1,3,128,128]{3,2,1,0:T(8,128)S(1)}, u32[]{:S(2)}, u32[]{:S(2)}) %collective-permute-start.18) | collective-permute-done | bytes 196640 | tf_op jit(solution)/shard_map/ppermute | solution.py:17
  271.1 3.4 fusion.29
  277.6 3.2 multiply_reduce_fusion
  280.8 39.2 %psum.31 = f32[128]{0:T(128)S(1)} all-reduce(f32[128]{0:T(128)S(1)} %get-tuple-element.4), channel_id=1, replica_groups=mesh['wide'=8,'narrow'=4] {'wide','narrow'}, use_global_device_ids=true, to_apply=%region_16.17 | all-reduce | flops 128 | bytes 1024 | tf_op jit(solution)/shard_map/psum | solution.py:99
  322.6 4.6 %collective-permute-start.20 = (f32[1,3,128,128]{3,2,1,0:T(8,128)S(1)}, f32[1,3,128,128]{3,2,1,0:T(8,128)S(1)}, u32[]{:S(2)}, u32[]{:S(2)}) collective-permute-start(f32[1,3,128,128]{3,2,1,0:T(8,128)S(1)} %get-tuple-element.15), channel_id=1, source_target_pairs={{0,1},{1,2},{2,3},{4,5},{5,6},{6,7},{8,9},{9,10},{10,11},{12,13},{... | collective-permute-start | bytes 589832 | tf_op jit(solution)/shard_map/ppermute | solution.py:17
  327.2 3.1 fusion.10
  330.9 7.6 %collective-permute-done.22 = f32[1,3,128,128]{3,2,1,0:T(8,128)S(1)} collective-permute-done((f32[1,3,128,128]{3,2,1,0:T(8,128)S(1)}, f32[1,3,128,128]{3,2,1,0:T(8,128)S(1)}, u32[]{:S(2)}, u32[]{:S(2)}) %collective-permute-start.22) | collective-permute-done | bytes 196640 | tf_op jit(solution)/shard_map/ppermute | solution.py:17
  (234 shorter events, 79.6 us)
Async XLA Ops:
  1.8 18.4 %collective-permute-start.3 = (bf16[1,3,128,128]{3,2,1,0:T(8,128)(2,1)S(1)}, bf16[1,3,128,128]{3,2,1,0:T(8,128)(2,1)}, u32[]{:S(2)}, u32[]{:S(2)}) collective-permute-start(bf16[1,3,128,128]{3,2,1,0:T(8,128)(2,1)S(1)} %get-tuple-element.33), channel_id=1, source_target_pairs={{4,0},{8,4},{12,8},{16,12},{20,16},{24,20},{28,24},{0,28},{5,1},{9... | collective-permute-start | bytes 294920 | tf_op jit(solution)/shard_map/ppermute | solution.py:20
  5.2 14.1 %collective-permute-start.2 = (bf16[1,3,128,128]{3,2,1,0:T(8,128)(2,1)S(1)}, bf16[1,3,128,128]{3,2,1,0:T(8,128)(2,1)}, u32[]{:S(2)}, u32[]{:S(2)}) collective-permute-start(bf16[1,3,128,128]{3,2,1,0:T(8,128)(2,1)S(1)} %get-tuple-element.34), channel_id=1, source_target_pairs={{0,4},{4,8},{8,12},{12,16},{16,20},{20,24},{24,28},{28,0},{1,5},{5... | collective-permute-start | bytes 294920 | tf_op jit(solution)/shard_map/ppermute | solution.py:17
  5.2 13.2 %collective-permute-start.1 = (bf16[1,3,128,128]{3,2,1,0:T(8,128)(2,1)S(1)}, bf16[1,3,128,128]{3,2,1,0:T(8,128)(2,1)}, u32[]{:S(2)}, u32[]{:S(2)}) collective-permute-start(bf16[1,3,128,128]{3,2,1,0:T(8,128)(2,1)S(1)} %get-tuple-element.35), channel_id=1, source_target_pairs={{1,0},{2,1},{3,2},{5,4},{6,5},{7,6},{9,8},{10,9},{11,10},{13,12},{... | collective-permute-start | bytes 294920 | tf_op jit(solution)/shard_map/ppermute | solution.py:20
  6.5 11.0 %collective-permute-start = (bf16[1,3,128,128]{3,2,1,0:T(8,128)(2,1)S(1)}, bf16[1,3,128,128]{3,2,1,0:T(8,128)(2,1)}, u32[]{:S(2)}, u32[]{:S(2)}) collective-permute-start(bf16[1,3,128,128]{3,2,1,0:T(8,128)(2,1)S(1)} %get-tuple-element.36), channel_id=1, source_target_pairs={{0,1},{1,2},{2,3},{4,5},{5,6},{6,7},{8,9},{9,10},{10,11},{12,13},{... | collective-permute-start | bytes 294920 | tf_op jit(solution)/shard_map/ppermute | solution.py:17
  33.1 6.4 %collective-permute-start.4 = (f32[1,3,128,128]{3,2,1,0:T(8,128)S(1)}, f32[1,3,128,128]{3,2,1,0:T(8,128)S(1)}, u32[]{:S(2)}, u32[]{:S(2)}) collective-permute-start(f32[1,3,128,128]{3,2,1,0:T(8,128)S(1)} %get-tuple-element.32), channel_id=1, source_target_pairs={{0,1},{1,2},{2,3},{4,5},{5,6},{6,7},{8,9},{9,10},{10,11},{12,13},{... | collective-permute-start | bytes 589832 | tf_op jit(solution)/shard_map/ppermute | solution.py:17
  35.9 8.1 %collective-permute-start.5 = (f32[1,3,128,128]{3,2,1,0:T(8,128)S(1)}, f32[1,3,128,128]{3,2,1,0:T(8,128)S(1)}, u32[]{:S(2)}, u32[]{:S(2)}) collective-permute-start(f32[1,3,128,128]{3,2,1,0:T(8,128)S(1)} %get-tuple-element.31), channel_id=1, source_target_pairs={{1,0},{2,1},{3,2},{5,4},{6,5},{7,6},{9,8},{10,9},{11,10},{13,12},{... | collective-permute-start | bytes 589832 | tf_op jit(solution)/shard_map/ppermute | solution.py:20
  37.2 7.9 %collective-permute-start.7 = (f32[1,3,128,128]{3,2,1,0:T(8,128)S(1)}, f32[1,3,128,128]{3,2,1,0:T(8,128)S(1)}, u32[]{:S(2)}, u32[]{:S(2)}) collective-permute-start(f32[1,3,128,128]{3,2,1,0:T(8,128)S(1)} %get-tuple-element.29), channel_id=1, source_target_pairs={{4,0},{8,4},{12,8},{16,12},{20,16},{24,20},{28,24},{0,28},{5,1},{9... | collective-permute-start | bytes 589832 | tf_op jit(solution)/shard_map/ppermute | solution.py:20
  39.1 6.0 %collective-permute-start.6 = (f32[1,3,128,128]{3,2,1,0:T(8,128)S(1)}, f32[1,3,128,128]{3,2,1,0:T(8,128)S(1)}, u32[]{:S(2)}, u32[]{:S(2)}) collective-permute-start(f32[1,3,128,128]{3,2,1,0:T(8,128)S(1)} %get-tuple-element.30), channel_id=1, source_target_pairs={{0,4},{4,8},{8,12},{12,16},{16,20},{20,24},{24,28},{28,0},{1,5},{5... | collective-permute-start | bytes 589832 | tf_op jit(solution)/shard_map/ppermute | solution.py:17
  88.5 5.7 %collective-permute-start.8 = (f32[1,3,128,128]{3,2,1,0:T(8,128)S(1)}, f32[1,3,128,128]{3,2,1,0:T(8,128)S(1)}, u32[]{:S(2)}, u32[]{:S(2)}) collective-permute-start(f32[1,3,128,128]{3,2,1,0:T(8,128)S(1)} %get-tuple-element.28), channel_id=1, source_target_pairs={{0,1},{1,2},{2,3},{4,5},{5,6},{6,7},{8,9},{9,10},{10,11},{12,13},{... | collective-permute-start | bytes 589832 | tf_op jit(solution)/shard_map/ppermute | solution.py:17
  91.0 7.6 %collective-permute-start.9 = (f32[1,3,128,128]{3,2,1,0:T(8,128)S(1)}, f32[1,3,128,128]{3,2,1,0:T(8,128)S(1)}, u32[]{:S(2)}, u32[]{:S(2)}) collective-permute-start(f32[1,3,128,128]{3,2,1,0:T(8,128)S(1)} %get-tuple-element.27), channel_id=1, source_target_pairs={{1,0},{2,1},{3,2},{5,4},{6,5},{7,6},{9,8},{10,9},{11,10},{13,12},{... | collective-permute-start | bytes 589832 | tf_op jit(solution)/shard_map/ppermute | solution.py:20
  92.3 7.3 %collective-permute-start.11 = (f32[1,3,128,128]{3,2,1,0:T(8,128)S(1)}, f32[1,3,128,128]{3,2,1,0:T(8,128)S(1)}, u32[]{:S(2)}, u32[]{:S(2)}) collective-permute-start(f32[1,3,128,128]{3,2,1,0:T(8,128)S(1)} %get-tuple-element.25), channel_id=1, source_target_pairs={{4,0},{8,4},{12,8},{16,12},{20,16},{24,20},{28,24},{0,28},{5,1},{9... | collective-permute-start | bytes 589832 | tf_op jit(solution)/shard_map/ppermute | solution.py:20
  92.3 7.2 %collective-permute-start.10 = (f32[1,3,128,128]{3,2,1,0:T(8,128)S(1)}, f32[1,3,128,128]{3,2,1,0:T(8,128)S(1)}, u32[]{:S(2)}, u32[]{:S(2)}) collective-permute-start(f32[1,3,128,128]{3,2,1,0:T(8,128)S(1)} %get-tuple-element.26), channel_id=1, source_target_pairs={{0,4},{4,8},{8,12},{12,16},{16,20},{20,24},{24,28},{28,0},{1,5},{5... | collective-permute-start | bytes 589832 | tf_op jit(solution)/shard_map/ppermute | solution.py:17
  113.6 48.3 %collective-permute-start.12 = (f32[1,3,128,128]{3,2,1,0:T(8,128)}, f32[1,3,128,128]{3,2,1,0:T(8,128)}, u32[]{:S(2)}, u32[]{:S(2)}) collective-permute-start(f32[1,3,128,128]{3,2,1,0:T(8,128)} %get-tuple-element.24), channel_id=1, source_target_pairs={{0,1},{1,2},{2,3},{4,5},{5,6},{6,7},{8,9},{9,10},{10,11},{12,13},{... | collective-permute-start | bytes 589832 | tf_op jit(solution)/shard_map/ppermute | solution.py:17
  118.9 43.9 %collective-permute-start.13 = (f32[1,3,128,128]{3,2,1,0:T(8,128)}, f32[1,3,128,128]{3,2,1,0:T(8,128)}, u32[]{:S(2)}, u32[]{:S(2)}) collective-permute-start(f32[1,3,128,128]{3,2,1,0:T(8,128)} %get-tuple-element.23), channel_id=1, source_target_pairs={{1,0},{2,1},{3,2},{5,4},{6,5},{7,6},{9,8},{10,9},{11,10},{13,12},{... | collective-permute-start | bytes 589832 | tf_op jit(solution)/shard_map/ppermute | solution.py:20
  120.2 44.5 %collective-permute-start.15 = (f32[1,3,128,128]{3,2,1,0:T(8,128)S(1)}, f32[1,3,128,128]{3,2,1,0:T(8,128)}, u32[]{:S(2)}, u32[]{:S(2)}) collective-permute-start(f32[1,3,128,128]{3,2,1,0:T(8,128)S(1)} %get-tuple-element.21), channel_id=1, source_target_pairs={{4,0},{8,4},{12,8},{16,12},{20,16},{24,20},{28,24},{0,28},{5,1},{9... | collective-permute-start | bytes 589832 | tf_op jit(solution)/shard_map/ppermute | solution.py:20
  120.3 43.5 %collective-permute-start.14 = (f32[1,3,128,128]{3,2,1,0:T(8,128)}, f32[1,3,128,128]{3,2,1,0:T(8,128)}, u32[]{:S(2)}, u32[]{:S(2)}) collective-permute-start(f32[1,3,128,128]{3,2,1,0:T(8,128)} %get-tuple-element.22), channel_id=1, source_target_pairs={{0,4},{4,8},{8,12},{12,16},{16,20},{20,24},{24,28},{28,0},{1,5},{5... | collective-permute-start | bytes 589832 | tf_op jit(solution)/shard_map/ppermute | solution.py:17
  213.2 45.0 %collective-permute-start.16 = (f32[1,3,128,128]{3,2,1,0:T(8,128)}, f32[1,3,128,128]{3,2,1,0:T(8,128)}, u32[]{:S(2)}, u32[]{:S(2)}) collective-permute-start(f32[1,3,128,128]{3,2,1,0:T(8,128)} %get-tuple-element.19), channel_id=1, source_target_pairs={{0,1},{1,2},{2,3},{4,5},{5,6},{6,7},{8,9},{9,10},{10,11},{12,13},{... | collective-permute-start | bytes 589832 | tf_op jit(solution)/shard_map/ppermute | solution.py:17
  215.5 43.6 %collective-permute-start.17 = (f32[1,3,128,128]{3,2,1,0:T(8,128)S(1)}, f32[1,3,128,128]{3,2,1,0:T(8,128)}, u32[]{:S(2)}, u32[]{:S(2)}) collective-permute-start(f32[1,3,128,128]{3,2,1,0:T(8,128)S(1)} %get-tuple-element.18), channel_id=1, source_target_pairs={{1,0},{2,1},{3,2},{5,4},{6,5},{7,6},{9,8},{10,9},{11,10},{13,12},{... | collective-permute-start | bytes 589832 | tf_op jit(solution)/shard_map/ppermute | solution.py:20
  257.2 9.0 %collective-permute-start.19 = (f32[1,3,128,128]{3,2,1,0:T(8,128)S(1)}, f32[1,3,128,128]{3,2,1,0:T(8,128)S(1)}, u32[]{:S(2)}, u32[]{:S(2)}) collective-permute-start(f32[1,3,128,128]{3,2,1,0:T(8,128)S(1)} %get-tuple-element.16), channel_id=1, source_target_pairs={{4,0},{8,4},{12,8},{16,12},{20,16},{24,20},{28,24},{0,28},{5,1},{9... | collective-permute-start | bytes 589832 | tf_op jit(solution)/shard_map/ppermute | solution.py:20
  258.1 8.0 %collective-permute-start.18 = (f32[1,3,128,128]{3,2,1,0:T(8,128)S(1)}, f32[1,3,128,128]{3,2,1,0:T(8,128)S(1)}, u32[]{:S(2)}, u32[]{:S(2)}) collective-permute-start(f32[1,3,128,128]{3,2,1,0:T(8,128)S(1)} %get-tuple-element.17), channel_id=1, source_target_pairs={{0,4},{4,8},{8,12},{12,16},{16,20},{20,24},{24,28},{28,0},{1,5},{5... | collective-permute-start | bytes 589832 | tf_op jit(solution)/shard_map/ppermute | solution.py:17
  321.3 9.6 %collective-permute-start.21 = (f32[1,3,128,128]{3,2,1,0:T(8,128)S(1)}, f32[1,3,128,128]{3,2,1,0:T(8,128)S(1)}, u32[]{:S(2)}, u32[]{:S(2)}) collective-permute-start(f32[1,3,128,128]{3,2,1,0:T(8,128)S(1)} %get-tuple-element.14), channel_id=1, source_target_pairs={{1,0},{2,1},{3,2},{5,4},{6,5},{7,6},{9,8},{10,9},{11,10},{13,12},{... | collective-permute-start | bytes 589832 | tf_op jit(solution)/shard_map/ppermute | solution.py:20
  322.6 8.3 %collective-permute-start.20 = (f32[1,3,128,128]{3,2,1,0:T(8,128)S(1)}, f32[1,3,128,128]{3,2,1,0:T(8,128)S(1)}, u32[]{:S(2)}, u32[]{:S(2)}) collective-permute-start(f32[1,3,128,128]{3,2,1,0:T(8,128)S(1)} %get-tuple-element.15), channel_id=1, source_target_pairs={{0,1},{1,2},{2,3},{4,5},{5,6},{6,7},{8,9},{9,10},{10,11},{12,13},{... | collective-permute-start | bytes 589832 | tf_op jit(solution)/shard_map/ppermute | solution.py:17
  330.3 8.1 %collective-permute-start.23 = (f32[1,3,128,128]{3,2,1,0:T(8,128)S(1)}, f32[1,3,128,128]{3,2,1,0:T(8,128)S(1)}, u32[]{:S(2)}, u32[]{:S(2)}) collective-permute-start(f32[1,3,128,128]{3,2,1,0:T(8,128)S(1)} %get-tuple-element.12), channel_id=1, source_target_pairs={{4,0},{8,4},{12,8},{16,12},{20,16},{24,20},{28,24},{0,28},{5,1},{9... | collective-permute-start | bytes 589832 | tf_op jit(solution)/shard_map/ppermute | solution.py:20
  330.7 7.8 %collective-permute-start.22 = (f32[1,3,128,128]{3,2,1,0:T(8,128)S(1)}, f32[1,3,128,128]{3,2,1,0:T(8,128)S(1)}, u32[]{:S(2)}, u32[]{:S(2)}) collective-permute-start(f32[1,3,128,128]{3,2,1,0:T(8,128)S(1)} %get-tuple-element.13), channel_id=1, source_target_pairs={{0,4},{4,8},{8,12},{12,16},{16,20},{20,24},{24,28},{28,0},{1,5},{5... | collective-permute-start | bytes 589832 | tf_op jit(solution)/shard_map/ppermute | solution.py:17
  (47 other events, 707.3 us)
